TPU v7x, 256 devices: a whole 4x4x8 slice. The times are simulated.
256 devices in a mesh: batch: 4 (over x_lo, core), seq: 64 (over y, x_hi, z).
Axes of the slice: x: 4 (x_hi: 2, x_lo: 2; x = x_hi * 2 + x_lo), y: 4, z: 8, core: 2. Of those that a mesh axis runs over, the one named last changes fastest.
Arguments:
- signal: bfloat16 [4, 16384, 256], P('batch', 'seq'), may hold values from -0.125 to 0.125
- grad_out: bfloat16 [4, 16384, 256], P('batch', 'seq'), may hold values from -6 to 6
- filter_taps: float32 [16384, 256], P('seq'), may hold values from -0.125 to 0.125
- skip_gain: float32 [256], replicated, may hold values from 0.5 to 2
Outputs:
- input_grad: bfloat16 [4, 16384, 256], P('batch', 'seq')
- filter_grad: float32 [16384, 256], P('seq')
All inputs are finite; a program needn't handle non-finite values.
Results may differ from a plain program's by a relative error of at most 0.001.
Values sent between devices are 32-bit elements; how exact they have to be, the bound alone decides.
A program may use at most 64 MiB of HBM per device.

v0:
```python
import jax
import jax.numpy as jnp
from jax import lax
from jax.sharding import PartitionSpec as P


def split_up(x, dim, devices):
    shape = x.shape
    parts = x.reshape(*shape[:dim], devices, shape[dim] // devices, *shape[dim + 1 :])
    return jnp.moveaxis(parts, dim, 0)


def summed_on_arrival(x, axis, dim):
    parts = split_up(x, dim, lax.axis_size(axis))
    arrived = lax.all_to_all(parts, axis, split_axis=0, concat_axis=0, tiled=True)
    return arrived.sum(axis=0)


def copy_for_each(x, axis):
    devices = lax.axis_size(axis)
    return lax.all_to_all(jnp.broadcast_to(x[None], (devices, *x.shape)), axis, 0, 0, tiled=True)


def in_order(parts, dim):
    shape = list(parts.shape[1:])
    shape[dim] *= parts.shape[0]
    return jnp.moveaxis(parts, 0, dim).reshape(shape)


def gather_directly(x, axis, dim):
    parts = copy_for_each(x, axis)
    return in_order(parts, dim)


def angle_table(height, width, period):
    product = lax.broadcasted_iota(jnp.int32, (height, width), 0) * lax.broadcasted_iota(
        jnp.int32, (height, width), 1
    )
    return 2.0 * jnp.pi / period * (product % period).astype(jnp.float32)


def angle_of(product, period):
    return 2.0 * jnp.pi / period * (product % period).astype(jnp.float32)


def coarse_order(slot, seq_count):
    pair_index = slot // 2
    odd_slot = slot % 2
    return jnp.where(
        pair_index == 0,
        odd_slot * seq_count,
        jnp.where(odd_slot == 0, pair_index, 2 * seq_count - pair_index),
    )


def contract(form, table, operand):
    return jnp.einsum(form, table, operand, precision=lax.Precision.HIGHEST)


def forward_spectra(columns):
    seq_count = lax.axis_size("seq")
    row_count = columns.shape[0]
    part_rows = row_count // seq_count
    period_len = 2 * row_count * seq_count
    spread = lax.all_to_all(
        columns.reshape(1, row_count, columns.shape[1]),
        "seq",
        split_axis=1,
        concat_axis=0,
        tiled=True,
    )
    slot_grid = lax.broadcasted_iota(jnp.int32, (2 * seq_count, seq_count), 0)
    source_grid = lax.broadcasted_iota(jnp.int32, (2 * seq_count, seq_count), 1)
    first_table = angle_of(coarse_order(slot_grid, seq_count) * source_grid, 2 * seq_count)
    cos_first = jnp.cos(first_table)
    sin_first = jnp.sin(first_table)
    half_width = spread.shape[2] // 2
    real_in = spread[:, :, :half_width]
    imag_in = spread[:, :, half_width:]
    real_part = contract("ks,srw->krw", cos_first, real_in) + contract(
        "ks,srw->krw", sin_first, imag_in
    )
    imag_part = contract("ks,srw->krw", cos_first, imag_in) - contract(
        "ks,srw->krw", sin_first, real_in
    )
    global_row = lax.axis_index("seq") * part_rows + lax.broadcasted_iota(
        jnp.int32, (2 * seq_count, part_rows), 1
    )
    coarse = coarse_order(lax.broadcasted_iota(jnp.int32, (2 * seq_count, part_rows), 0), seq_count)
    phases = angle_of(global_row * coarse, period_len)
    cos_turn = jnp.cos(phases)[:, :, None]
    sin_turn = jnp.sin(phases)[:, :, None]
    rotated = jnp.stack(
        [real_part * cos_turn + imag_part * sin_turn, imag_part * cos_turn - real_part * sin_turn]
    )
    inner_table = angle_table(row_count, row_count, row_count)
    cos_inner = jnp.cos(inner_table)
    sin_inner = jnp.sin(inner_table)
    pieces = lax.all_to_all(rotated, "seq", split_axis=1, concat_axis=2, tiled=True)
    real_sum = contract("qr,krw->kqw", cos_inner, pieces[0]) + contract(
        "qr,krw->kqw", sin_inner, pieces[1]
    )
    imag_sum = contract("qr,krw->kqw", cos_inner, pieces[1]) - contract(
        "qr,krw->kqw", sin_inner, pieces[0]
    )
    return jnp.stack([real_sum, imag_sum])


def split_pairs(packed):
    reversed_q = packed[:, :, ::-1]
    zero_row = jnp.roll(reversed_q[:, 0], 1, axis=1)
    own_pair = jnp.stack([zero_row, reversed_q[:, 1]], axis=1)
    partner = jnp.where(lax.axis_index("seq") == 0, own_pair, reversed_q[:, ::-1])
    first = jnp.stack([0.5 * (packed[0] + partner[0]), 0.5 * (packed[1] - partner[1])])
    second = jnp.stack([0.5 * (packed[1] + partner[1]), 0.5 * (partner[0] - packed[0])])
    return (first, second)


def inverse_rows(spectra):
    seq_count = lax.axis_size("seq")
    row_count = spectra.shape[2]
    period_len = 2 * row_count * seq_count
    inner_table = angle_table(row_count, row_count, row_count)
    cos_inner = jnp.cos(inner_table)
    sin_inner = jnp.sin(inner_table)
    real_sum = contract("qr,krw->kqw", cos_inner, spectra[0]) - contract(
        "qr,krw->kqw", sin_inner, spectra[1]
    )
    imag_sum = contract("qr,krw->kqw", cos_inner, spectra[1]) + contract(
        "qr,krw->kqw", sin_inner, spectra[0]
    )
    coarse = coarse_order(
        2 * lax.axis_index("seq") + lax.broadcasted_iota(jnp.int32, (2, row_count), 0), seq_count
    )
    position = lax.broadcasted_iota(jnp.int32, (2, row_count), 1)
    phases = angle_of(position * coarse, period_len)
    cos_turn = jnp.cos(phases)[:, :, None]
    sin_turn = jnp.sin(phases)[:, :, None]
    rotated = jnp.stack(
        [real_sum * cos_turn - imag_sum * sin_turn, real_sum * sin_turn + imag_sum * cos_turn]
    )
    target_grid = lax.broadcasted_iota(jnp.int32, (seq_count, 2 * seq_count), 0)
    slot_grid = lax.broadcasted_iota(jnp.int32, (seq_count, 2 * seq_count), 1)
    last_table = angle_of(target_grid * coarse_order(slot_grid, seq_count), 2 * seq_count)
    cos_last = jnp.cos(last_table)
    sin_last = jnp.sin(last_table)
    pieces = lax.all_to_all(rotated, "seq", split_axis=2, concat_axis=1, tiled=True)
    value = contract("sk,krw->srw", cos_last, pieces[0]) - contract(
        "sk,krw->srw", sin_last, pieces[1]
    )
    other = contract("sk,krw->srw", sin_last, pieces[0]) + contract(
        "sk,krw->srw", cos_last, pieces[1]
    )
    gathered = (value / period_len, other / period_len)
    gathered = jnp.concatenate([gathered[0], gathered[1]], axis=2)
    home_rows = lax.all_to_all(gathered, "seq", split_axis=0, concat_axis=1, tiled=True)
    return home_rows.reshape(row_count, home_rows.shape[2])


def invert_all(spectra):
    half_width = spectra.shape[3] // 2
    joined = jnp.stack(
        [
            spectra[0, :, :, :half_width] - spectra[1, :, :, half_width:],
            spectra[1, :, :, :half_width] + spectra[0, :, :, half_width:],
        ]
    )
    return inverse_rows(joined)


def shards(signal, grad_out, filter_taps, skip_gain):
    channels = filter_taps.shape[1]
    signal_rows = signal[0].astype(jnp.float32)
    grad_rows = grad_out[0].astype(jnp.float32)
    tap_half = filter_taps.shape[1] // 2
    columns = jnp.concatenate(
        [signal_rows, filter_taps[:, :tap_half], grad_rows, filter_taps[:, tap_half:]], axis=1
    )
    first, second = split_pairs(forward_spectra(columns))
    signal_spec = first[:, :, :, :channels]
    grad_spec = second[:, :, :, :channels]
    own_spec = jnp.concatenate([first[:, :, :, channels:], second[:, :, :, channels:]], axis=3)
    input_spec = jnp.stack(
        [
            grad_spec[0] * own_spec[0] + grad_spec[1] * own_spec[1],
            grad_spec[1] * own_spec[0] - grad_spec[0] * own_spec[1],
        ]
    )
    filter_terms = jnp.stack(
        [
            grad_spec[0] * signal_spec[0] + grad_spec[1] * signal_spec[1],
            grad_spec[1] * signal_spec[0] - grad_spec[0] * signal_spec[1],
        ]
    )
    shared_terms = summed_on_arrival(filter_terms, "batch", 3)
    rows_back = invert_all(jnp.concatenate([input_spec, shared_terms], axis=3))
    filter_grad = gather_directly(rows_back[:, channels:], "batch", 1)
    input_grad = (rows_back[:, :channels] + skip_gain[None, :] * grad_rows).astype(jnp.bfloat16)
    return (input_grad[None], filter_grad)


def solution(mesh):
    return jax.shard_map(
        shards,
        mesh=mesh,
        in_specs=(P("batch", "seq", None), P("batch", "seq", None), P("seq", None), P()),
        out_specs=(P("batch", "seq", None), P("seq", None)),
        check_vma=False,
    )
```

profile of v0, /device:TPU:1, one launch (start us, length us, event | category | flops | bytes accessed | tf_op | source)
XLA Modules:
  0.0 239.2 jit_solution(16720733413574259168)
XLA Ops:
  0.6 1.0 fusion.173
  1.6 1.0 bitcast_convert_fusion
  2.7 1.7 copy.29
  4.4 15.1 %all-to-all-start = ((f32[1,256,768]{2,0,1:T(1,128)}), f32[1,256,768]{2,0,1:T(1,128)S(1)}, u32[]{:S(2)}, u32[]{:S(2)}) async-start(f32[1,256,768]{2,0,1:T(1,128)} %copy.29), calls=%async_computation | async-start | bytes 1572864 | tf_op jit(solution)/shard_map/all_to_all | solution.py:65
  19.7 21.7 %all-to-all-done = f32[1,256,768]{2,0,1:T(1,128)S(1)} async-done(((f32[1,256,768]{2,0,1:T(1,128)}), f32[1,256,768]{2,0,1:T(1,128)S(1)}, u32[]{:S(2)}, u32[]{:S(2)}) %all-to-all-start) | async-done | bytes 786464 | tf_op jit(solution)/shard_map/all_to_all | solution.py:65
  41.4 1.9 reduce
  46.5 1.1 add_bitcast_fusion
  47.8 2.2 copy.32
  50.0 8.2 %all-to-all-start.1 = ((f32[2,128,4,384]{3,2,0,1:T(4,128)}), f32[2,128,4,384]{3,2,0,1:T(4,128)S(1)}, u32[]{:S(2)}, u32[]{:S(2)}) async-start(f32[2,128,4,384]{3,2,0,1:T(4,128)} %copy.32), calls=%async_computation.1 | async-start | bytes 3145728 | tf_op jit(solution)/shard_map/all_to_all | solution.py:99
  58.2 37.3 %all-to-all-done.1 = f32[2,128,4,384]{3,2,0,1:T(4,128)S(1)} async-done(((f32[2,128,4,384]{3,2,0,1:T(4,128)}), f32[2,128,4,384]{3,2,0,1:T(4,128)S(1)}, u32[]{:S(2)}, u32[]{:S(2)}) %all-to-all-start.1) | async-done | bytes 1572896 | tf_op jit(solution)/shard_map/all_to_all | solution.py:99
  97.4 1.8 fusion.35
  99.6 1.8 fusion.37
  101.4 1.8 convolution_add_fusion
  103.2 1.8 convolution_subtract_fusion
  105.0 1.3 fusion.4
  106.3 7.2 %slice.129 = f32[2,1,256,384]{2,3,0,1:T(8,128)} reverse(f32[2,1,256,384]{2,3,0,1:T(8,128)} %get-tuple-element.22), dimensions={2} | reverse | bytes 1572864 | tf_op jit(solution)/shard_map/slice | solution.py:111
  113.5 1.2 slice.158
  114.7 7.2 %slice.133 = f32[2,1,256,384]{2,3,1,0:T(8,128)} reverse(f32[2,1,256,384]{2,3,1,0:T(8,128)} %get-tuple-element.23), dimensions={2} | reverse | bytes 1572864 | tf_op jit(solution)/shard_map/slice | solution.py:112
  121.9 8.7 %rev.4 = f32[2,2,256,384]{2,3,1,0:T(8,128)} reverse(f32[2,2,256,384]{2,3,1,0:T(8,128)S(1)} %pad_maximum_fusion), dimensions={1,2} | reverse | bytes 3145728 | tf_op jit(solution)/shard_map/rev | solution.py:113
  130.6 1.5 maximum_bitcast_fusion.1
  132.3 1.3 maximum_select_fusion
  134.3 1.1 copy_bitcast_fusion.1
  135.4 8.5 %all-to-all-start.2 = ((f32[4,2,2,256,64]{3,4,2,1,0:T(8,128)}), f32[4,2,2,256,64]{3,4,2,1,0:T(8,128)S(1)}, u32[]{:S(2)}, u32[]{:S(2)}) async-start(f32[4,2,2,256,64]{3,4,2,1,0:T(8,128)} %copy_bitcast_fusion.1), calls=%async_computation.2 | async-start | bytes 2097152 | tf_op jit(solution)/shard_map/all_to_all | solution.py:15
  144.2 13.2 %all-to-all-done.2 = f32[4,2,2,256,64]{3,4,2,1,0:T(8,128)S(1)} async-done(((f32[4,2,2,256,64]{3,4,2,1,0:T(8,128)}), f32[4,2,2,256,64]{3,4,2,1,0:T(8,128)S(1)}, u32[]{:S(2)}, u32[]{:S(2)}) %all-to-all-start.2) | async-done | bytes 1048608 | tf_op jit(solution)/shard_map/all_to_all | solution.py:15
  157.6 1.4 fusion.31
  159.0 1.4 fusion.33
  160.4 1.4 convolution_add_fusion.2
  161.9 1.5 subtract_bitcast_fusion.1
  164.0 32.6 %all_to_all.61 = f32[2,2,256,160]{3,1,0,2:T(2,128)S(1)} all-to-all(f32[2,2,256,160]{3,1,0,2:T(2,128)S(1)} %copy.41), channel_id=1, replica_groups=mesh['batch'=4,'seq'=64] {'seq'}, dimensions={2} | all-to-all | bytes 1310720 | tf_op jit(solution)/shard_map/all_to_all | solution.py:147
  202.0 22.7 %all_to_all.62 = f32[64,4,320]{2,1,0:T(4,128)S(1)} all-to-all(f32[64,4,320]{2,1,0:T(4,128)S(1)} %copy.49), channel_id=1, replica_groups=mesh['batch'=4,'seq'=64] {'seq'}, dimensions={0} | all-to-all | bytes 655360 | tf_op jit(solution)/shard_map/all_to_all | solution.py:156
  225.6 7.7 %all-to-all-start.5 = ((f32[4,256,64]{1,2,0:T(8,128)}), f32[4,256,64]{1,2,0:T(8,128)S(1)}, u32[]{:S(2)}, u32[]{:S(2)}) async-start(f32[4,256,64]{1,2,0:T(8,128)} %broadcast_in_dim.5), calls=%async_computation.5 | async-start | bytes 524288 | tf_op jit(solution)/shard_map/all_to_all | solution.py:21
  234.0 4.3 %all-to-all-done.5 = f32[4,256,64]{1,2,0:T(8,128)S(1)} async-done(((f32[4,256,64]{1,2,0:T(8,128)}), f32[4,256,64]{1,2,0:T(8,128)S(1)}, u32[]{:S(2)}, u32[]{:S(2)}) %all-to-all-start.5) | async-done | bytes 262176 | tf_op jit(solution)/shard_map/all_to_all | solution.py:21
  (61 shorter events, 15.5 us)
Async XLA Ops:
  4.4 37.0 %all-to-all-start = ((f32[1,256,768]{2,0,1:T(1,128)}), f32[1,256,768]{2,0,1:T(1,128)S(1)}, u32[]{:S(2)}, u32[]{:S(2)}) async-start(f32[1,256,768]{2,0,1:T(1,128)} %copy.29), calls=%async_computation | async-start | bytes 1572864 | tf_op jit(solution)/shard_map/all_to_all | solution.py:65
  19.6 26.9 %copy-start.2 = (s32[128]{0:T(128)}, s32[128]{0:T(128)S(1)}, u32[]{:S(2)}) copy-start(s32[128]{0:T(128)S(1)} %get-tuple-element.44) | copy-start | bytes 1540
  19.6 26.9 %copy-start.4 = (s32[128]{0:T(128)}, s32[128]{0:T(128)S(1)}, u32[]{:S(2)}) copy-start(s32[128]{0:T(128)S(1)} %get-tuple-element.45) | copy-start | bytes 1540
  50.0 45.6 %all-to-all-start.1 = ((f32[2,128,4,384]{3,2,0,1:T(4,128)}), f32[2,128,4,384]{3,2,0,1:T(4,128)S(1)}, u32[]{:S(2)}, u32[]{:S(2)}) async-start(f32[2,128,4,384]{3,2,0,1:T(4,128)} %copy.32), calls=%async_computation.1 | async-start | bytes 3145728 | tf_op jit(solution)/shard_map/all_to_all | solution.py:99
  130.6 1.6 copy-start
  135.4 22.0 %all-to-all-start.2 = ((f32[4,2,2,256,64]{3,4,2,1,0:T(8,128)}), f32[4,2,2,256,64]{3,4,2,1,0:T(8,128)S(1)}, u32[]{:S(2)}, u32[]{:S(2)}) async-start(f32[4,2,2,256,64]{3,4,2,1,0:T(8,128)} %copy_bitcast_fusion.1), calls=%async_computation.2 | async-start | bytes 2097152 | tf_op jit(solution)/shard_map/all_to_all | solution.py:15
  197.0 0.8 copy-start.3
  197.0 0.8 copy-start.5
  202.0 31.3 %copy-start.1 = (bf16[1,256,256]{2,1,0:T(8,128)(2,1)S(1)}, bf16[1,256,256]{2,1,0:T(8,128)(2,1)}, u32[]{:S(2)}) copy-start(bf16[1,256,256]{2,1,0:T(8,128)(2,1)} %param.5) | copy-start | bytes 393220
  202.0 31.3 %copy-start.6 = (f32[256]{0:T(256)S(1)}, f32[256]{0:T(256)}, u32[]{:S(2)}) copy-start(f32[256]{0:T(256)} %param.7) | copy-start | bytes 3076
  225.6 12.7 %all-to-all-start.5 = ((f32[4,256,64]{1,2,0:T(8,128)}), f32[4,256,64]{1,2,0:T(8,128)S(1)}, u32[]{:S(2)}, u32[]{:S(2)}) async-start(f32[4,256,64]{1,2,0:T(8,128)} %broadcast_in_dim.5), calls=%async_computation.5 | async-start | bytes 524288 | tf_op jit(solution)/shard_map/all_to_all | solution.py:21
where the time goes:
time: 241 us; the launch traced here: 239 us
  waiting for transfers between devices  76.6 us (32%)
  blocking collectives  55.3 us (23%)
  starting transfers between devices  39.6 us (16%)
  local copies, waits for them, and re-layouts  36.1 us (15%)
  matrix products  20.2 us (8%)
  other arithmetic  10.4 us (4%)
    all_to_all x1, waiting for transfers between devices, forward_spectra(): lax.all_to_all(rotated, 'seq', split_axis=1, concat_axis=2, tiled=True)  37.3 us
    all_to_all x1, blocking collectives, inverse_rows(): lax.all_to_all(rotated, 'seq', split_axis=2, concat_axis=1, tiled=True)  32.6 us
    all_to_all x1, blocking collectives, inverse_rows(): lax.all_to_all(gathered, 'seq', split_axis=0, concat_axis=1, tiled=True)  22.7 us
    all_to_all x1, waiting for transfers between devices, forward_spectra(): lax.all_to_all(columns.reshape(1, row_count, columns.shape[1]), 'seq', sp...  21.7 us
    dot_general x16, matrix products, contract(): return jnp.einsum(form, table, operand, precision=lax.Precision.HIGHEST)  20.2 us
    all_to_all x1, starting transfers between devices, forward_spectra(): lax.all_to_all(columns.reshape(1, row_count, columns.shape[1]), 'seq', sp...  15.1 us
    all_to_all x1, waiting for transfers between devices, summed_on_arrival(): lax.all_to_all(parts, axis, split_axis=0, concat_axis=0, tiled=True)  13.2 us
    rev x1, local copies, waits for them, and re-layouts, split_pairs(): reversed_q[:, ::-1]  8.74 us
  transfers between devices with their start and end apart: 4, of which 4 were waited for; matrix products, arithmetic and copies ran while one was open for 0% of the time, Pallas kernels for 0%

commit v1 on v0

--- a/solution.py
+++ b/solution.py
@@ -1,7 +1,18 @@
+import functools
 import jax
 import jax.numpy as jnp
 from jax import lax
 from jax.sharding import PartitionSpec as P
+from jax.lax import all_to_all, axis_size
+
+
+def work_modes(vals, axis_name):
+    return jnp.concatenate(
+        all_to_all(jnp.stack(jnp.split(vals, axis_size(axis_name), 1)), axis_name, 0, 0), 0
+    )
+
+
+_point_block = functools.partial(work_modes, axis_name="seq")
 
 
 def split_up(x, dim, devices):
@@ -62,13 +73,7 @@
     row_count = columns.shape[0]
     part_rows = row_count // seq_count
     period_len = 2 * row_count * seq_count
-    spread = lax.all_to_all(
-        columns.reshape(1, row_count, columns.shape[1]),
-        "seq",
-        split_axis=1,
-        concat_axis=0,
-        tiled=True,
-    )
+    spread = _point_block(columns.reshape(1, row_count, columns.shape[1]))
     slot_grid = lax.broadcasted_iota(jnp.int32, (2 * seq_count, seq_count), 0)
     source_grid = lax.broadcasted_iota(jnp.int32, (2 * seq_count, seq_count), 1)
     first_table = angle_of(coarse_order(slot_grid, seq_count) * source_grid, 2 * seq_count)

time: 241 us -> 275 us (1.14)
  local copies, waits for them, and re-layouts: 36.1 us -> 72.7 us
    unnamed x15 -> x78, local copies, waits for them, and re-layouts: 1 us -> 38.8 us
where the time goes in v1:
time: 275 us; the launch traced here: 274 us
  waiting for transfers between devices  76.6 us (28%)
  local copies, waits for them, and re-layouts  72.7 us (26%)
  blocking collectives  55.3 us (20%)
  starting transfers between devices  39.6 us (14%)
  matrix products  20.2 us (7%)
  other arithmetic  8.48 us (3%)
    unnamed x78, local copies, waits for them, and re-layouts  38.8 us
    all_to_all x1, waiting for transfers between devices, forward_spectra(): lax.all_to_all(rotated, 'seq', split_axis=1, concat_axis=2, tiled=True)  37.3 us
    all_to_all x1, blocking collectives, inverse_rows(): lax.all_to_all(rotated, 'seq', split_axis=2, concat_axis=1, tiled=True)  32.6 us
    all_to_all x1, blocking collectives, inverse_rows(): lax.all_to_all(gathered, 'seq', split_axis=0, concat_axis=1, tiled=True)  22.7 us
    all_to_all x1, waiting for transfers between devices, work_modes(): all_to_all(jnp.stack(jnp.split(vals, axis_size(axis_name), 1)), axis_name...  21.7 us
    dot_general x16, matrix products, contract(): return jnp.einsum(form, table, operand, precision=lax.Precision.HIGHEST)  20.2 us
    all_to_all x1, starting transfers between devices, work_modes(): all_to_all(jnp.stack(jnp.split(vals, axis_size(axis_name), 1)), axis_name...  15.1 us
    all_to_all x1, waiting for transfers between devices, summed_on_arrival(): lax.all_to_all(parts, axis, split_axis=0, concat_axis=0, tiled=True)  13.2 us
  transfers between devices with their start and end apart: 4, of which 4 were waited for; matrix products, arithmetic and copies ran while one was open for 0% of the time, Pallas kernels for 0%

profile of v1, /device:TPU:1, one launch (start us, length us, event | category | flops | bytes accessed | tf_op | source)
XLA Modules:
  0.0 273.9 jit_solution(12642059580337318563)
XLA Ops:
  0.6 1.0 fusion.172
  1.6 1.0 bitcast_convert_fusion
  41.1 15.1 %all-to-all-start = ((f32[64,1,4,768]{3,2,1,0:T(4,128)}), f32[64,1,4,768]{3,2,1,0:T(4,128)S(1)}, u32[]{:S(2)}, u32[]{:S(2)}) async-start(f32[64,1,4,768]{3,2,1,0:T(4,128)} %constant_dynamic-update-slice_fusion), calls=%async_computation | async-start | bytes 1572864 | tf_op jit(solution)/shard_map/all_to_all | solution.py:11
  56.4 21.7 %all-to-all-done = f32[64,1,4,768]{3,2,1,0:T(4,128)S(1)} async-done(((f32[64,1,4,768]{3,2,1,0:T(4,128)}), f32[64,1,4,768]{3,2,1,0:T(4,128)S(1)}, u32[]{:S(2)}, u32[]{:S(2)}) %all-to-all-start) | async-done | bytes 786464 | tf_op jit(solution)/shard_map/all_to_all | solution.py:11
  79.2 1.0 fusion.18
  80.2 1.0 convolution_subtract_fusion.1
  81.2 1.1 add_bitcast_fusion
  82.4 2.2 copy.29
  84.7 8.2 %all-to-all-start.1 = ((f32[2,128,4,384]{3,2,0,1:T(4,128)}), f32[2,128,4,384]{3,2,0,1:T(4,128)S(1)}, u32[]{:S(2)}, u32[]{:S(2)}) async-start(f32[2,128,4,384]{3,2,0,1:T(4,128)} %copy.29), calls=%async_computation.1 | async-start | bytes 3145728 | tf_op jit(solution)/shard_map/all_to_all | solution.py:104
  92.9 37.3 %all-to-all-done.1 = f32[2,128,4,384]{3,2,0,1:T(4,128)S(1)} async-done(((f32[2,128,4,384]{3,2,0,1:T(4,128)}), f32[2,128,4,384]{3,2,0,1:T(4,128)S(1)}, u32[]{:S(2)}, u32[]{:S(2)}) %all-to-all-start.1) | async-done | bytes 1572896 | tf_op jit(solution)/shard_map/all_to_all | solution.py:104
  132.1 1.8 fusion.35
  134.3 1.8 fusion.37
  136.1 1.8 convolution_add_fusion
  137.9 1.8 convolution_subtract_fusion
  139.7 1.3 fusion.4
  141.0 7.2 %slice.129 = f32[2,1,256,384]{2,3,0,1:T(8,128)} reverse(f32[2,1,256,384]{2,3,0,1:T(8,128)} %get-tuple-element.22), dimensions={2} | reverse | bytes 1572864 | tf_op jit(solution)/shard_map/slice | solution.py:116
  148.2 1.2 slice.158
  149.4 7.2 %slice.133 = f32[2,1,256,384]{2,3,1,0:T(8,128)} reverse(f32[2,1,256,384]{2,3,1,0:T(8,128)} %get-tuple-element.23), dimensions={2} | reverse | bytes 1572864 | tf_op jit(solution)/shard_map/slice | solution.py:117
  156.6 8.8 %rev.4 = f32[2,2,256,384]{2,3,1,0:T(8,128)} reverse(f32[2,2,256,384]{2,3,1,0:T(8,128)S(1)} %pad_maximum_fusion), dimensions={1,2} | reverse | bytes 3145728 | tf_op jit(solution)/shard_map/rev | solution.py:118
  165.4 1.5 maximum_bitcast_fusion.1
  167.0 1.3 maximum_select_fusion
  169.1 1.1 copy_bitcast_fusion.1
  170.2 8.5 %all-to-all-start.2 = ((f32[4,2,2,256,64]{3,4,2,1,0:T(8,128)}), f32[4,2,2,256,64]{3,4,2,1,0:T(8,128)S(1)}, u32[]{:S(2)}, u32[]{:S(2)}) async-start(f32[4,2,2,256,64]{3,4,2,1,0:T(8,128)} %copy_bitcast_fusion.1), calls=%async_computation.2 | async-start | bytes 2097152 | tf_op jit(solution)/shard_map/all_to_all | solution.py:26
  178.9 13.2 %all-to-all-done.2 = f32[4,2,2,256,64]{3,4,2,1,0:T(8,128)S(1)} async-done(((f32[4,2,2,256,64]{3,4,2,1,0:T(8,128)}), f32[4,2,2,256,64]{3,4,2,1,0:T(8,128)S(1)}, u32[]{:S(2)}, u32[]{:S(2)}) %all-to-all-start.2) | async-done | bytes 1048608 | tf_op jit(solution)/shard_map/all_to_all | solution.py:26
  192.3 1.4 fusion.31
  193.8 1.4 fusion.33
  195.2 1.4 convolution_add_fusion.2
  196.6 1.4 subtract_bitcast_fusion.1
  198.7 32.6 %all_to_all.54 = f32[2,2,256,160]{3,1,0,2:T(2,128)S(1)} all-to-all(f32[2,2,256,160]{3,1,0,2:T(2,128)S(1)} %copy.38), channel_id=1, replica_groups=mesh['batch'=4,'seq'=64] {'seq'}, dimensions={2} | all-to-all | bytes 1310720 | tf_op jit(solution)/shard_map/all_to_all | solution.py:152
  236.7 22.7 %all_to_all.55 = f32[64,4,320]{2,1,0:T(4,128)S(1)} all-to-all(f32[64,4,320]{2,1,0:T(4,128)S(1)} %copy.46), channel_id=1, replica_groups=mesh['batch'=4,'seq'=64] {'seq'}, dimensions={0} | all-to-all | bytes 655360 | tf_op jit(solution)/shard_map/all_to_all | solution.py:161
  260.4 7.7 %all-to-all-start.5 = ((f32[4,256,64]{1,2,0:T(8,128)}), f32[4,256,64]{1,2,0:T(8,128)S(1)}, u32[]{:S(2)}, u32[]{:S(2)}) async-start(f32[4,256,64]{1,2,0:T(8,128)} %broadcast_in_dim.5), calls=%async_computation.5 | async-start | bytes 524288 | tf_op jit(solution)/shard_map/all_to_all | solution.py:32
  268.7 4.3 %all-to-all-done.5 = f32[4,256,64]{1,2,0:T(8,128)S(1)} async-done(((f32[4,256,64]{1,2,0:T(8,128)}), f32[4,256,64]{1,2,0:T(8,128)S(1)}, u32[]{:S(2)}, u32[]{:S(2)}) %all-to-all-start.5) | async-done | bytes 262176 | tf_op jit(solution)/shard_map/all_to_all | solution.py:32
  (122 shorter events, 51.8 us)
Async XLA Ops:
  41.1 37.0 %all-to-all-start = ((f32[64,1,4,768]{3,2,1,0:T(4,128)}), f32[64,1,4,768]{3,2,1,0:T(4,128)S(1)}, u32[]{:S(2)}, u32[]{:S(2)}) async-start(f32[64,1,4,768]{3,2,1,0:T(4,128)} %constant_dynamic-update-slice_fusion), calls=%async_computation | async-start | bytes 1572864 | tf_op jit(solution)/shard_map/all_to_all | solution.py:11
  56.3 24.9 %copy-start.2 = (s32[128]{0:T(128)}, s32[128]{0:T(128)S(1)}, u32[]{:S(2)}) copy-start(s32[128]{0:T(128)S(1)} %get-tuple-element.42) | copy-start | bytes 1540
  56.3 24.9 %copy-start.4 = (s32[128]{0:T(128)}, s32[128]{0:T(128)S(1)}, u32[]{:S(2)}) copy-start(s32[128]{0:T(128)S(1)} %get-tuple-element.43) | copy-start | bytes 1540
  84.7 45.6 %all-to-all-start.1 = ((f32[2,128,4,384]{3,2,0,1:T(4,128)}), f32[2,128,4,384]{3,2,0,1:T(4,128)S(1)}, u32[]{:S(2)}, u32[]{:S(2)}) async-start(f32[2,128,4,384]{3,2,0,1:T(4,128)} %copy.29), calls=%async_computation.1 | async-start | bytes 3145728 | tf_op jit(solution)/shard_map/all_to_all | solution.py:104
  165.4 1.6 copy-start
  170.2 22.0 %all-to-all-start.2 = ((f32[4,2,2,256,64]{3,4,2,1,0:T(8,128)}), f32[4,2,2,256,64]{3,4,2,1,0:T(8,128)S(1)}, u32[]{:S(2)}, u32[]{:S(2)}) async-start(f32[4,2,2,256,64]{3,4,2,1,0:T(8,128)} %copy_bitcast_fusion.1), calls=%async_computation.2 | async-start | bytes 2097152 | tf_op jit(solution)/shard_map/all_to_all | solution.py:26
  231.7 0.8 copy-start.3
  231.7 0.8 copy-start.5
  236.7 31.4 %copy-start.1 = (bf16[1,256,256]{2,1,0:T(8,128)(2,1)S(1)}, bf16[1,256,256]{2,1,0:T(8,128)(2,1)}, u32[]{:S(2)}) copy-start(bf16[1,256,256]{2,1,0:T(8,128)(2,1)} %param.5) | copy-start | bytes 393220
  236.7 31.4 %copy-start.6 = (f32[256]{0:T(256)S(1)}, f32[256]{0:T(256)}, u32[]{:S(2)}) copy-start(f32[256]{0:T(256)} %param.7) | copy-start | bytes 3076
  260.4 12.7 %all-to-all-start.5 = ((f32[4,256,64]{1,2,0:T(8,128)}), f32[4,256,64]{1,2,0:T(8,128)S(1)}, u32[]{:S(2)}, u32[]{:S(2)}) async-start(f32[4,256,64]{1,2,0:T(8,128)} %broadcast_in_dim.5), calls=%async_computation.5 | async-start | bytes 524288 | tf_op jit(solution)/shard_map/all_to_all | solution.py:32
